TPU v7x, 32 devices: a whole 2x2x4 slice. The times are simulated.
32 devices in a mesh: tok: 4 (over x, core), col: 8 (over z, y).
Axes of the slice: x: 2, y: 2, z: 4, core: 2. Of those that a mesh axis runs over, the one named last changes fastest.
Arguments:
- hidden_in: bfloat16 [1024, 36864], P('tok', 'col'), may hold values from -6 to 6
- down_weight: bfloat16 [4608, 36864], P('col', 'tok'), may hold values from -0.046875 to 0.046875
- keep_mask: int32 [4608, 36864], P('col', 'tok'), may hold values 0 or 1
Outputs:
- layer_out: bfloat16 [1024, 4608], P(('tok', 'col'))
- hessian: float32 [4608, 4608], P('col', 'tok')
All inputs are finite; a program needn't handle non-finite values. No bound on the sum of `keep_mask` on one device may be relied on, other than what follows from the above.
Results may differ from a plain program's by a relative error of at most 0.012.
Values may be sent and summed in bfloat16 or wider, within the bound.
No kernel may reach another device: no remote copies, remote signals or barrier semaphores. Data moves between devices by JAX's collectives and lax.ppermute only.
A program may use at most 192 MiB of HBM per device.

v0:
```python
import jax
import jax.numpy as jnp
from jax import lax
from jax.sharding import PartitionSpec as P


def contract_rows(left, right):
    return lax.dot_general(
        left, right, (((0,), (0,)), ((), ())), preferred_element_type=jnp.float32
    )


def contract_last(left, right):
    return lax.dot_general(
        left, right, (((1,), (1,)), ((), ())), preferred_element_type=jnp.float32
    )


def body(hidden_in, down_weight, keep_mask):
    pruned = down_weight * keep_mask.astype(down_weight.dtype)
    all_features = lax.all_gather(hidden_in, "col", axis=1, tiled=True)
    summed = contract_last(all_features, lax.all_gather(pruned, "tok", axis=1, tiled=True))
    layer_cols = summed.astype(jnp.bfloat16)
    scaling = 2.0 / (layer_cols.shape[0] * lax.axis_size("tok"))
    layer_out = lax.all_to_all(layer_cols, "col", split_axis=0, concat_axis=1, tiled=True)
    hessian_term = contract_rows(layer_cols, lax.all_gather(layer_cols, "col", axis=1, tiled=True))
    hessian = lax.psum_scatter(
        (hessian_term * scaling).astype(jnp.bfloat16), "tok", scatter_dimension=1, tiled=True
    ).astype(jnp.float32)
    return (layer_out, hessian)


def solution(mesh):
    in_specs = (P("tok", "col"), P("col", "tok"), P("col", "tok"))
    out_specs = (P(("tok", "col"), None), P("col", "tok"))
    return jax.shard_map(body, mesh=mesh, in_specs=in_specs, out_specs=out_specs, check_vma=False)
```

profile of v0, /device:TPU:0, one launch (start us, length us, event | category | flops | bytes accessed | tf_op | source)
XLA Modules:
  0.0 784.0 jit_solution(10702195190926574698)
XLA Ops:
  7.2 0.0 all-gather.6.cloned.1.call-start
  7.2 0.7 all-gather.6.cloned.1.call-update
  7.9 0.0 all-gather.4.cloned.1.call-start
  7.9 15.3 %convert_multiply_fusion = bf16[576,9216]{1,0:T(8,128)(2,1)} fusion(bf16[576,9216]{1,0:T(8,128)(2,1)} %param.4, s32[576,9216]{1,0:T(8,128)} %param.5), kind=kLoop, calls=%fused_computation.1 | loop fusion | flops 10616832 | bytes 42467328 | tf_op jit(solution)/shard_map/mul | solution.py:20
  23.2 0.0 all-gather.4.cloned.1.call-update
  23.3 0.0 all-gather.8.cloned.1.call-start
  23.3 351.4 %all-gather.6.cloned.1.call-done = bf16[256,36864]{1,0:T(8,128)(2,1)} async-done(((bf16[256,4608]{1,0:T(8,128)(2,1)}), bf16[256,36864]{1,0:T(8,128)(2,1)}) %all-gather.6.cloned.1.call-update) | async-done | bytes 18874384 | tf_op jit(solution)/shard_map/all_gather | solution.py:21
  374.7 254.7 %all-gather.4.cloned.1.call-done = bf16[576,36864]{1,0:T(8,128)(2,1)} async-done(((bf16[576,9216]{1,0:T(8,128)(2,1)}), bf16[576,36864]{1,0:T(8,128)(2,1)}) %all-gather.4.cloned.1.call-update) | async-done | bytes 42467344 | tf_op jit(solution)/shard_map/all_gather | solution.py:22
  629.4 23.3 %convolution_convert_fusion = bf16[576,256]{1,0:T(8,128)(2,1)} fusion(bf16[576,36864]{1,0:T(8,128)(2,1)} %all-gather.4.cloned.1.call-done, bf16[256,36864]{1,0:T(8,128)(2,1)} %all-gather.6.cloned.1.call-done), kind=kOutput, calls=%fused_computation.2 | convolution fusion | flops 10871783424 | bytes 61636608 | tf_op jit(solution)/shard_map/dot_general | solution.py:14
  652.7 0.0 all-gather.8.cloned.1.call-update
  652.8 0.0 reduce-scatter.4.cloned.1.call-start
  652.8 51.9 %all-gather.8.cloned.1.call-done = bf16[256,4608]{0,1:T(8,128)(2,1)} async-done(((bf16[256,576]{0,1:T(8,128)(2,1)}), bf16[256,4608]{0,1:T(8,128)(2,1)}) %all-gather.8.cloned.1.call-update) | async-done | bytes 2359312 | tf_op jit(solution)/shard_map/all_gather | solution.py:26
  704.7 5.8 multiply_convert_fusion
  710.5 0.0 copy-start
  710.5 8.4 %copy.11 = bf16[576,4608]{0,1:T(8,128)(2,1)} copy(bf16[576,4608]{1,0:T(8,128)(2,1)} %multiply_convert_fusion) | data formatting | bytes 10616832
  718.9 0.0 reduce-scatter.4.cloned.1.call-update
  719.0 0.0 copy-done
  719.0 0.2 copy.9
  719.2 13.3 %all_to_all.19 = bf16[8,32,576]{2,1,0:T(8,128)(2,1)S(1)} all-to-all(bf16[8,32,576]{2,1,0:T(8,128)(2,1)S(1)} %bitcast.13), channel_id=1, replica_groups=mesh['tok'=4,'col'=8] {'col'}, dimensions={0} | all-to-all | bytes 589824 | tf_op jit(solution)/shard_map/all_to_all | solution.py:25
  732.5 0.1 copy.10
  732.6 1.0 all_to_all.17
  733.6 40.3 %reduce-scatter.4.cloned.1.call-done = bf16[1152,576]{1,0:T(8,128)(2,1)} async-done(((bf16[4608,576]{1,0:T(8,128)(2,1)}), bf16[1152,576]{1,0:T(8,128)(2,1)}) %reduce-scatter.4.cloned.1.call-update) | async-done | bytes 1327120
  773.8 1.9 copy.12
  775.7 1.7 convert_element_type.19
Async XLA Ops:
  7.2 367.5 %all-gather.6.cloned.1.call-start = ((), (), s32[]{:S(2)}) async-start(), calls=%async_computation.3 | async-start | bytes 21233664 | tf_op jit(solution)/shard_map/all_gather | solution.py:21
  7.9 621.5 %all-gather.4.cloned.1.call-start = ((), (), s32[]{:S(2)}) async-start(), calls=%async_computation.2 | async-start | bytes 53084160 | tf_op jit(solution)/shard_map/all_gather | solution.py:22
  23.3 681.5 %all-gather.8.cloned.1.call-start = ((), (), s32[]{:S(2)}) async-start(), calls=%async_computation.4 | async-start | bytes 2654208 | tf_op jit(solution)/shard_map/all_gather | solution.py:26
  652.8 121.1 %reduce-scatter.4.cloned.1.call-start = ((), (), s32[]{:S(2)}) async-start(), calls=%async_computation.5 | async-start | bytes 7372800
  710.5 8.5 %copy-start = (bf16[576,256]{1,0:T(8,128)(2,1)S(1)}, bf16[576,256]{1,0:T(8,128)(2,1)}, u32[]{:S(2)}) copy-start(bf16[576,256]{1,0:T(8,128)(2,1)} %convolution_convert_fusion) | copy-start | bytes 884740
Sparse Core Ops, SparseCore 0:
  9.5 365.1 all-gather.5
  376.2 253.1 all-gather.3
  652.9 51.8 all-gather.7
  719.1 54.7 reduce-scatter.3
where the time goes:
time: 784 us
  waiting for transfers between devices  699 us (89%)
  matrix products  29.1 us (4%)
  other arithmetic  17 us (2%)
  between operations  13.8 us (2%)
  blocking collectives  13.3 us (2%)
  local copies, waits for them, and re-layouts  11.6 us (1%)
    all_gather x1, waiting for transfers between devices, body(): all_features = lax.all_gather(hidden_in, 'col', axis=1, tiled=True)  351 us
    all_gather x1, waiting for transfers between devices, body(): lax.all_gather(pruned, 'tok', axis=1, tiled=True)  255 us
    all_gather x1, waiting for transfers between devices, body(): lax.all_gather(layer_cols, 'col', axis=1, tiled=True)  51.9 us
    unnamed x5, waiting for transfers between devices  41 us
    dot_general x1, matrix products, contract_last(): lax.dot_general(left, right, (((1,), (1,)), ((), ())), preferred_element_...  23.3 us
  transfers between devices with their start and end apart: 4, of which 4 were waited for; matrix products, arithmetic and copies ran while one was open for 2% of the time, Pallas kernels for 0%

commit v1 on v0

--- a/solution.py
+++ b/solution.py
@@ -18,7 +18,12 @@
 
 def body(hidden_in, down_weight, keep_mask):
     pruned = down_weight * keep_mask.astype(down_weight.dtype)
-    all_features = lax.all_gather(hidden_in, "col", axis=1, tiled=True)
+    ring = [hidden_in]
+    for hop in range(7):
+        ring.append(lax.ppermute(ring[-1], "col", [(dev, (dev + 1) % 8) for dev in range(8)]))
+    all_features = jnp.roll(
+        jnp.concatenate(ring[::-1], axis=1), (lax.axis_index("col") + 1) * ring[0].shape[1], axis=1
+    )
     summed = contract_last(all_features, lax.all_gather(pruned, "tok", axis=1, tiled=True))
     layer_cols = summed.astype(jnp.bfloat16)
     scaling = 2.0 / (layer_cols.shape[0] * lax.axis_size("tok"))

time: 784 us -> 597 us (0.76)
  waiting for transfers between devices: 699 us -> 460 us
  local copies, waits for them, and re-layouts: 11.6 us -> 60 us
    ppermute x0 -> x7, waiting for transfers between devices: none -> 372 us  [body(): lax.ppermute(ring[-1], 'col', [(dev, (dev + 1) % 8) for dev in range(8)])]
    all_gather x1 -> x0, waiting for transfers between devices: 351 us -> none  [body(): all_features = lax.all_gather(hidden_in, 'col', axis=1, tiled=True)]
    all_gather x1, waiting for transfers between devices: 255 us -> 0.01 us  [body(): lax.all_gather(pruned, 'tok', axis=1, tiled=True)]
    unnamed x4 -> x39, local copies, waits for them, and re-layouts: 10.3 us -> 56.2 us
    unnamed x5 -> x4, waiting for transfers between devices: 41 us -> 39.4 us
  transfers between devices with their start and end apart: 4 -> 10, of which waited for: 4 -> 9; matrix products, arithmetic and copies ran while one was open for 2% -> 7% of each run, Pallas kernels for 0% -> 0%
where the time goes in v1:
time: 597 us; the launch traced here: 596 us
  waiting for transfers between devices  460 us (77%)
  local copies, waits for them, and re-layouts  60 us (10%)
  matrix products  29.2 us (5%)
  other arithmetic  16.4 us (3%)
  between operations  13.8 us (2%)
  blocking collectives  13.3 us (2%)
    ppermute x7, waiting for transfers between devices, body(): lax.ppermute(ring[-1], 'col', [(dev, (dev + 1) % 8) for dev in range(8)])  372 us
    unnamed x39, local copies, waits for them, and re-layouts  56.2 us
    all_gather x1, waiting for transfers between devices, body(): lax.all_gather(layer_cols, 'col', axis=1, tiled=True)  48.2 us
    unnamed x4, waiting for transfers between devices  39.4 us
    dot_general x1, matrix products, contract_last(): lax.dot_general(left, right, (((1,), (1,)), ((), ())), preferred_element_...  23.4 us
    mul x1, other arithmetic, body(): pruned = down_weight * keep_mask.astype(down_weight.dtype)  14.7 us
    all_to_all x1, blocking collectives, body(): lax.all_to_all(layer_cols, 'col', split_axis=0, concat_axis=1, tiled=True)  13.3 us
  transfers between devices with their start and end apart: 10, of which 9 were waited for; matrix products, arithmetic and copies ran while one was open for 7% of the time, Pallas kernels for 0%

profile of v1, /device:TPU:0, one launch (start us, length us, event | category | flops | bytes accessed | tf_op | source)
XLA Modules:
  0.0 596.0 jit_solution(3892642806917026979)
XLA Ops:
  7.2 0.0 copy-start
  7.2 0.0 all-gather.3.cloned.1.call-start
  7.2 14.7 %convert_multiply_fusion = bf16[576,9216]{1,0:T(8,128)(2,1)} fusion(bf16[576,9216]{1,0:T(8,128)(2,1)} %param.4, s32[576,9216]{1,0:T(8,128)} %param.5), kind=kLoop, calls=%fused_computation.3 | loop fusion | flops 10616832 | bytes 42467328 | tf_op jit(solution)/shard_map/mul | solution.py:20
  22.0 0.0 all-gather.3.cloned.1.call-update
  22.0 0.0 all-gather.5.cloned.1.call-start
  22.0 0.0 copy-done
  22.0 3.0 collective-permute-start
  25.1 54.3 %collective-permute-done = bf16[256,4608]{1,0:T(8,128)(2,1)S(1)} collective-permute-done((bf16[256,4608]{1,0:T(8,128)(2,1)S(1)}, bf16[256,4608]{1,0:T(8,128)(2,1)S(1)}, u32[]{:S(2)}, u32[]{:S(2)}) %collective-permute-start) | collective-permute-done | bytes 2359328 | tf_op jit(solution)/shard_map/ppermute | solution.py:23
  79.4 0.0 copy-start.1
  79.4 1.5 copy-done.1
  80.8 0.0 collective-permute-start.1
  80.8 55.1 %collective-permute-done.1 = bf16[256,4608]{1,0:T(8,128)(2,1)S(1)} collective-permute-done((bf16[256,4608]{1,0:T(8,128)(2,1)S(1)}, bf16[256,4608]{1,0:T(8,128)(2,1)S(1)}, u32[]{:S(2)}, u32[]{:S(2)}) %collective-permute-start.1) | collective-permute-done | bytes 2359328 | tf_op jit(solution)/shard_map/ppermute | solution.py:23
  136.0 0.0 copy-start.3
  136.0 1.4 copy-done.3
  137.4 0.0 collective-permute-start.2
  137.4 54.2 %collective-permute-done.2 = bf16[256,4608]{1,0:T(8,128)(2,1)S(1)} collective-permute-done((bf16[256,4608]{1,0:T(8,128)(2,1)S(1)}, bf16[256,4608]{1,0:T(8,128)(2,1)S(1)}, u32[]{:S(2)}, u32[]{:S(2)}) %collective-permute-start.2) | collective-permute-done | bytes 2359328 | tf_op jit(solution)/shard_map/ppermute | solution.py:23
  191.6 1.5 copy-done.5
  193.1 0.0 collective-permute-start.3
  193.1 53.4 %collective-permute-done.3 = bf16[256,4608]{1,0:T(8,128)(2,1)S(1)} collective-permute-done((bf16[256,4608]{1,0:T(8,128)(2,1)S(1)}, bf16[256,4608]{1,0:T(8,128)(2,1)S(1)}, u32[]{:S(2)}, u32[]{:S(2)}) %collective-permute-start.3) | collective-permute-done | bytes 2359328 | tf_op jit(solution)/shard_map/ppermute | solution.py:23
  246.5 1.4 copy-done.7
  247.9 0.0 collective-permute-start.4
  247.9 52.5 %collective-permute-done.4 = bf16[256,4608]{1,0:T(8,128)(2,1)S(1)} collective-permute-done((bf16[256,4608]{1,0:T(8,128)(2,1)S(1)}, bf16[256,4608]{1,0:T(8,128)(2,1)S(1)}, u32[]{:S(2)}, u32[]{:S(2)}) %collective-permute-start.4) | collective-permute-done | bytes 2359328 | tf_op jit(solution)/shard_map/ppermute | solution.py:23
  300.5 1.4 copy-done.9
  301.9 0.0 collective-permute-start.5
  301.9 51.8 %collective-permute-done.5 = bf16[256,4608]{1,0:T(8,128)(2,1)} collective-permute-done((bf16[256,4608]{1,0:T(8,128)(2,1)S(1)}, bf16[256,4608]{1,0:T(8,128)(2,1)}, u32[]{:S(2)}, u32[]{:S(2)}) %collective-permute-start.5) | collective-permute-done | bytes 2359328 | tf_op jit(solution)/shard_map/ppermute | solution.py:23
  353.7 0.0 collective-permute-start.6
  353.7 0.0 copy-start.4
  353.7 0.0 copy-start.2
  353.7 51.1 %collective-permute-done.6 = bf16[256,4608]{1,0:T(8,128)(2,1)} collective-permute-done((bf16[256,4608]{1,0:T(8,128)(2,1)}, bf16[256,4608]{1,0:T(8,128)(2,1)}, u32[]{:S(2)}, u32[]{:S(2)}) %collective-permute-start.6) | collective-permute-done | bytes 2359328 | tf_op jit(solution)/shard_map/ppermute | solution.py:23
  404.8 3.2 constant_dynamic-update-slice_fusion.15
  408.0 3.2 constant_dynamic-update-slice_fusion.14
  411.3 3.2 constant_dynamic-update-slice_fusion.13
  414.5 3.3 constant_dynamic-update-slice_fusion.12
  417.8 3.2 constant_dynamic-update-slice_fusion.11
  421.0 3.2 constant_dynamic-update-slice_fusion.10
  424.3 3.3 constant_dynamic-update-slice_fusion.9
  427.5 1.6 constant_dynamic-update-slice_fusion.8
  429.1 3.2 constant_dynamic-update-slice_fusion.7
  432.3 3.2 constant_dynamic-update-slice_fusion.6
  435.6 0.0 copy-done.10
  435.6 1.6 constant_dynamic-update-slice_fusion.5
  437.2 0.0 copy-done.8
  437.2 1.6 constant_dynamic-update-slice_fusion.4
  438.8 0.0 copy-done.6
  438.8 1.6 constant_dynamic-update-slice_fusion.3
  440.4 0.0 copy-done.4
  440.4 1.6 constant_dynamic-update-slice_fusion.2
  442.0 0.0 copy-done.2
  442.0 1.6 constant_dynamic-update-slice_fusion.1
  443.6 1.6 constant_dynamic-update-slice_fusion
  445.1 23.4 %fusion.2 = bf16[256,576]{0,1:T(8,128)(2,1)} fusion(bf16[576,36864]{1,0:T(8,128)(2,1)} %all-gather.3.cloned.1.call-done, bf16[256,73728]{1,0:T(8,128)(2,1)} %constant_dynamic-update-slice_fusion, s32[]{:T(128)S(6)} %select_n.14), kind=kOutput, calls=%fused_computation.4 | convolution fusion | flops 10871783424 | bytes 61636612 | tf_op jit(solution)/shard_map/dot_general | solution.py:14
  468.6 0.0 all-gather.5.cloned.1.call-update
  468.6 0.0 reduce-scatter.4.cloned.1.call-start
  468.6 48.2 %all-gather.5.cloned.1.call-done = bf16[256,4608]{0,1:T(8,128)(2,1)} async-done(((bf16[256,576]{0,1:T(8,128)(2,1)}), bf16[256,4608]{0,1:T(8,128)(2,1)}) %all-gather.5.cloned.1.call-update) | async-done | bytes 2359312 | tf_op jit(solution)/shard_map/all_gather | solution.py:31
  516.8 5.8 multiply_convert_fusion
  522.6 8.4 %copy.11 = bf16[576,4608]{0,1:T(8,128)(2,1)} copy(bf16[576,4608]{1,0:T(8,128)(2,1)} %multiply_convert_fusion) | data formatting | bytes 10616832
  531.0 0.0 reduce-scatter.4.cloned.1.call-update
  531.0 1.2 copy.9
  532.2 13.3 %all_to_all.19 = bf16[8,32,576]{2,1,0:T(8,128)(2,1)S(1)} all-to-all(bf16[8,32,576]{2,1,0:T(8,128)(2,1)S(1)} %bitcast.9), channel_id=1, replica_groups=mesh['tok'=4,'col'=8] {'col'}, dimensions={0} | all-to-all | bytes 589824 | tf_op jit(solution)/shard_map/all_to_all | solution.py:30
  545.5 0.1 copy.10
  545.6 1.0 all_to_all.17
  546.6 39.3 %reduce-scatter.4.cloned.1.call-done = bf16[1152,576]{1,0:T(8,128)(2,1)} async-done(((bf16[4608,576]{1,0:T(8,128)(2,1)}), bf16[1152,576]{1,0:T(8,128)(2,1)}) %reduce-scatter.4.cloned.1.call-update) | async-done | bytes 1327120
  585.9 1.9 copy.12
  587.8 1.7 convert_element_type.15
  (7 shorter events, 0.0 us)
Async XLA Ops:
  7.2 14.9 %copy-start = (bf16[256,4608]{1,0:T(8,128)(2,1)S(1)}, bf16[256,4608]{1,0:T(8,128)(2,1)}, u32[]{:S(2)}) copy-start(bf16[256,4608]{1,0:T(8,128)(2,1)} %param.3) | copy-start | bytes 7077892
  7.2 437.9 %all-gather.3.cloned.1.call-start = ((), (), s32[]{:S(2)}) async-start(), calls=%async_computation.2 | async-start | bytes 53084160 | tf_op jit(solution)/shard_map/all_gather | solution.py:27
  22.0 494.9 %all-gather.5.cloned.1.call-start = ((), (), s32[]{:S(2)}) async-start(), calls=%async_computation.3 | async-start | bytes 2654208 | tf_op jit(solution)/shard_map/all_gather | solution.py:31
  22.0 57.3 %collective-permute-start = (bf16[256,4608]{1,0:T(8,128)(2,1)S(1)}, bf16[256,4608]{1,0:T(8,128)(2,1)S(1)}, u32[]{:S(2)}, u32[]{:S(2)}) collective-permute-start(bf16[256,4608]{1,0:T(8,128)(2,1)S(1)} %copy-done), channel_id=1, source_target_pairs={{0,1},{1,2},{2,3},{3,4},{4,5},{5,6},{6,7},{7,0},{8,9},{9,10},{10,1... | collective-permute-start | bytes 7077896 | tf_op jit(solution)/shard_map/ppermute | solution.py:23
  79.4 1.5 copy-start.1
  80.8 55.1 %collective-permute-start.1 = (bf16[256,4608]{1,0:T(8,128)(2,1)S(1)}, bf16[256,4608]{1,0:T(8,128)(2,1)S(1)}, u32[]{:S(2)}, u32[]{:S(2)}) collective-permute-start(bf16[256,4608]{1,0:T(8,128)(2,1)S(1)} %collective-permute-done), channel_id=1, source_target_pairs={{0,1},{1,2},{2,3},{3,4},{4,5},{5,6},{6,7},{7,0},{8,9},{9,10},{10,1... | collective-permute-start | bytes 7077896 | tf_op jit(solution)/shard_map/ppermute | solution.py:23
  136.0 1.4 copy-start.3
  137.4 54.3 %collective-permute-start.2 = (bf16[256,4608]{1,0:T(8,128)(2,1)S(1)}, bf16[256,4608]{1,0:T(8,128)(2,1)S(1)}, u32[]{:S(2)}, u32[]{:S(2)}) collective-permute-start(bf16[256,4608]{1,0:T(8,128)(2,1)S(1)} %collective-permute-done.1), channel_id=1, source_target_pairs={{0,1},{1,2},{2,3},{3,4},{4,5},{5,6},{6,7},{7,0},{8,9},{9,10},{10,1... | collective-permute-start | bytes 7077896 | tf_op jit(solution)/shard_map/ppermute | solution.py:23
  191.6 1.5 copy-start.5
  193.1 53.4 %collective-permute-start.3 = (bf16[256,4608]{1,0:T(8,128)(2,1)S(1)}, bf16[256,4608]{1,0:T(8,128)(2,1)S(1)}, u32[]{:S(2)}, u32[]{:S(2)}) collective-permute-start(bf16[256,4608]{1,0:T(8,128)(2,1)S(1)} %collective-permute-done.2), channel_id=1, source_target_pairs={{0,1},{1,2},{2,3},{3,4},{4,5},{5,6},{6,7},{7,0},{8,9},{9,10},{10,1... | collective-permute-start | bytes 7077896 | tf_op jit(solution)/shard_map/ppermute | solution.py:23
  246.5 1.4 copy-start.7
  247.9 52.5 %collective-permute-start.4 = (bf16[256,4608]{1,0:T(8,128)(2,1)S(1)}, bf16[256,4608]{1,0:T(8,128)(2,1)S(1)}, u32[]{:S(2)}, u32[]{:S(2)}) collective-permute-start(bf16[256,4608]{1,0:T(8,128)(2,1)S(1)} %collective-permute-done.3), channel_id=1, source_target_pairs={{0,1},{1,2},{2,3},{3,4},{4,5},{5,6},{6,7},{7,0},{8,9},{9,10},{10,1... | collective-permute-start | bytes 7077896 | tf_op jit(solution)/shard_map/ppermute | solution.py:23
  300.5 1.4 copy-start.9
  301.9 51.8 %collective-permute-start.5 = (bf16[256,4608]{1,0:T(8,128)(2,1)S(1)}, bf16[256,4608]{1,0:T(8,128)(2,1)}, u32[]{:S(2)}, u32[]{:S(2)}) collective-permute-start(bf16[256,4608]{1,0:T(8,128)(2,1)S(1)} %collective-permute-done.4), channel_id=1, source_target_pairs={{0,1},{1,2},{2,3},{3,4},{4,5},{5,6},{6,7},{7,0},{8,9},{9,10},{10,1... | collective-permute-start | bytes 7077896 | tf_op jit(solution)/shard_map/ppermute | solution.py:23
  353.7 51.1 %collective-permute-start.6 = (bf16[256,4608]{1,0:T(8,128)(2,1)}, bf16[256,4608]{1,0:T(8,128)(2,1)}, u32[]{:S(2)}, u32[]{:S(2)}) collective-permute-start(bf16[256,4608]{1,0:T(8,128)(2,1)} %collective-permute-done.5), channel_id=1, source_target_pairs={{0,1},{1,2},{2,3},{3,4},{4,5},{5,6},{6,7},{7,0},{8,9},{9,10},{10,1... | collective-permute-start | bytes 7077896 | tf_op jit(solution)/shard_map/ppermute | solution.py:23
  353.7 81.9 %copy-start.10 = (bf16[256,4608]{1,0:T(8,128)(2,1)S(1)}, bf16[256,4608]{1,0:T(8,128)(2,1)}, u32[]{:S(2)}) copy-start(bf16[256,4608]{1,0:T(8,128)(2,1)} %copy-done.9) | copy-start | bytes 7077892
  353.7 83.5 %copy-start.8 = (bf16[256,4608]{1,0:T(8,128)(2,1)S(1)}, bf16[256,4608]{1,0:T(8,128)(2,1)}, u32[]{:S(2)}) copy-start(bf16[256,4608]{1,0:T(8,128)(2,1)} %copy-done.7) | copy-start | bytes 7077892
  353.7 85.1 %copy-start.6 = (bf16[256,4608]{1,0:T(8,128)(2,1)S(1)}, bf16[256,4608]{1,0:T(8,128)(2,1)}, u32[]{:S(2)}) copy-start(bf16[256,4608]{1,0:T(8,128)(2,1)} %copy-done.5) | copy-start | bytes 7077892
  353.7 86.7 %copy-start.4 = (bf16[256,4608]{1,0:T(8,128)(2,1)S(1)}, bf16[256,4608]{1,0:T(8,128)(2,1)}, u32[]{:S(2)}) copy-start(bf16[256,4608]{1,0:T(8,128)(2,1)} %copy-done.3) | copy-start | bytes 7077892
  353.7 88.3 %copy-start.2 = (bf16[256,4608]{1,0:T(8,128)(2,1)S(1)}, bf16[256,4608]{1,0:T(8,128)(2,1)}, u32[]{:S(2)}) copy-start(bf16[256,4608]{1,0:T(8,128)(2,1)} %copy-done.1) | copy-start | bytes 7077892
  468.6 117.3 %reduce-scatter.4.cloned.1.call-start = ((), (), s32[]{:S(2)}) async-start(), calls=%async_computation.4 | async-start | bytes 7372800
Sparse Core Ops, SparseCore 0:
  22.1 255.8 all-gather.2
  468.7 48.0 all-gather.4
  531.1 54.7 reduce-scatter.3
